TPU v7x, 32 devices: a whole 2x2x4 slice. The times are simulated.
32 devices in a mesh: aa: 8 (over y, x, core), ba: 4 (over z).
Axes of the slice: x: 2, y: 2, z: 4, core: 2. Of those that a mesh axis runs over, the one named last changes fastest.
Arguments:
- images: float32 [32, 4, 128, 4096], P(('aa', 'ba')), may hold values from 0 to 0.06, as said below
- depth: int32 [32], replicated, may hold values from 0 to 31, as said below
- brick_map: int32 [32], replicated, may hold values from 0 to 31, as said below
Outputs:
- composite: float32 [4, 128, 4096], replicated
Inputs may be any that keep to these rules, and one draw needn't show every extreme that they name: depth: a permutation of 0 to 31; the devices that share one index of ba hold bricks of 8 consecutive depth ranks. brick_map: a permutation of 0 to 31. images: channel 3 (alpha) lies between 0.002 and 0.06; channels 0 to 2 lie between 0 and the pixel's alpha.
All inputs are finite; a program needn't handle non-finite values.
Results may differ from a plain program's by a relative error of at most 0.00002.
Values sent between devices are 32-bit elements; how exact they have to be, the bound alone decides.
A program may use at most 128 MiB of HBM per device.

v0:
```python
import jax
import jax.numpy as jnp
from jax import lax
from jax.sharding import PartitionSpec as P


def blend_ordered(stacked, ordering):
    channels = stacked.shape[0]
    count = stacked.shape[1]
    rows = stacked.shape[2]
    columns = stacked.shape[3]
    ordered = jnp.take(stacked, ordering, axis=1)
    layers = jnp.moveaxis(ordered.reshape(channels, count, rows * columns), 1, 0)
    while layers.shape[0] > 1:
        front = layers[0::2]
        behind = layers[1::2]
        layers = front + (1.0 - front[:, 3:4]) * behind
    return layers[0].reshape(channels, rows, columns)


def local(images, depth, brick_map):
    picture = images[0]
    count_a = lax.axis_size("aa")
    count_b = lax.axis_size("ba")
    devices = count_a * count_b
    rows = picture.shape[1]
    columns = picture.shape[2]
    bricks = jnp.arange(devices, dtype=jnp.int32)
    matches = brick_map[:, None] == bricks[None, :]
    device_rank = jnp.sum(jnp.where(matches, depth[None, :], 0), axis=1)
    rank_table = device_rank.reshape(count_a, count_b)
    index_b = lax.axis_index("ba")
    bands = picture.reshape(4, count_a, rows // count_a, columns)
    received = lax.all_to_all(bands, "aa", split_axis=1, concat_axis=1, tiled=True)
    group_ranks = lax.dynamic_index_in_dim(rank_table, index_b, 1, keepdims=False)
    partial_value = blend_ordered(received, jnp.argsort(group_ranks))
    pieces = partial_value.reshape(4, count_b, rows // devices, columns)
    second = lax.all_to_all(pieces, "ba", split_axis=1, concat_axis=1, tiled=True)
    group_front = jnp.min(rank_table, axis=0)
    strip = blend_ordered(second, jnp.argsort(group_front))
    return lax.all_gather(strip, ("aa", "ba"), axis=1, tiled=True)


def solution(mesh):
    placed = (P(("aa", "ba"), None, None, None), P(), P())
    return jax.shard_map(local, mesh=mesh, in_specs=placed, out_specs=P(), check_vma=False)
```

profile of v0, /device:TPU:0, one launch (start us, length us, event | category | flops | bytes accessed | tf_op | source)
XLA Modules:
  0.0 281.2 jit_solution(16213214686071297865)
XLA Ops:
  6.5 7.8 %copy.8 = f32[4,8,16,4096]{3,2,0,1:T(8,128)} copy(f32[4,8,16,4096]{3,2,1,0:T(8,128)} %bitcast.26) | data formatting | bytes 16777216 | tf_op jit(solution)/shard_map/reshape;squeeze | solution.py:33
  14.3 0.0 copy-start.1
  14.3 0.0 copy-start.2
  14.3 5.3 %all-to-all-start = ((f32[4,8,16,4096]{3,2,0,1:T(8,128)}), f32[4,8,16,4096]{3,2,0,1:T(8,128)}, u32[]{:S(2)}, u32[]{:S(2)}) async-start(f32[4,8,16,4096]{3,2,0,1:T(8,128)} %copy.8), calls=%async_computation | async-start | bytes 16777216 | tf_op jit(solution)/shard_map/all_to_all | solution.py:34
  19.6 0.0 copy-done.1
  19.6 0.0 copy-done.2
  19.7 0.2 select_reduce_fusion
  19.8 0.1 reshape.23
  19.9 0.2 dynamic-slice_reduce_fusion
  20.1 0.9 sort.35
  21.1 93.1 %all-to-all-done = f32[4,8,16,4096]{3,2,0,1:T(8,128)} async-done(((f32[4,8,16,4096]{3,2,0,1:T(8,128)}), f32[4,8,16,4096]{3,2,0,1:T(8,128)}, u32[]{:S(2)}, u32[]{:S(2)}) %all-to-all-start) | async-done | bytes 8388640 | tf_op jit(solution)/shard_map/all_to_all | solution.py:34
  114.1 7.9 %gather_fusion = f32[8,4,16,4096]{3,2,1,0:T(8,128)} fusion(f32[4,8,16,4096]{3,2,0,1:T(8,128)} %all-to-all-done, s32[1024]{0:T(1024)S(1)} %pad_clamp_fusion.1), kind=kCustom, calls=%fused_computation | custom fusion | bytes 16777248 | tf_op jit(solution)/shard_map/jit(_take)/gather | solution.py:12
  122.0 10.9 %gather.13 = f32[4,8,65536]{2,0,1:T(4,128)} reshape(f32[4,8,16,4096]{3,2,0,1:T(8,128)} %bitcast.25) | data formatting | bytes 16777216 | tf_op jit(solution)/shard_map/jit(_take)/gather | solution.py:12
  132.9 9.0 %select_bitcast_fusion = f32[8,4,65536]{2,1,0:T(4,128)} fusion(f32[4,8,65536]{2,0,1:T(4,128)} %gather.13, pred[8]{0:T(512)(128)(4,1)S(1)} %compare_and_fusion), kind=kLoop, calls=%fused_computation.2 | loop fusion | flops 2097152 | bytes 16777224 | tf_op jit(solution)/shard_map/transpose | solution.py:13
  141.9 0.0 copy-start
  141.9 2.6 slice.51
  144.5 1.4 slice_subtract_fusion
  145.9 0.7 copy.17
  146.6 0.0 copy-done
  146.6 1.6 multiply_add_fusion
  148.1 0.1 slice.54
  148.3 0.7 slice_subtract_fusion.1
  149.0 0.4 copy.18
  149.4 0.8 multiply_add_fusion.1
  150.2 0.3 slice_subtract_fusion.2
  150.6 0.4 fusion
  151.0 0.9 reshape_reshape_squeeze.3
  151.9 1.0 copy.9
  152.9 5.7 %all-to-all-start.1 = ((f32[4,4,4,4096]{3,2,0,1:T(4,128)}), f32[4,4,4,4096]{3,2,0,1:T(4,128)S(1)}, u32[]{:S(2)}, u32[]{:S(2)}) async-start(f32[4,4,4,4096]{3,2,0,1:T(4,128)} %copy.9), calls=%async_computation.1 | async-start | bytes 2097152 | tf_op jit(solution)/shard_map/all_to_all | solution.py:38
  158.6 0.0 all-gather.2.cloned.1.call-start
  158.6 0.8 sort.34
  159.5 21.9 %all-to-all-done.1 = f32[4,4,4,4096]{3,2,0,1:T(4,128)S(1)} async-done(((f32[4,4,4,4096]{3,2,0,1:T(4,128)}), f32[4,4,4,4096]{3,2,0,1:T(4,128)S(1)}, u32[]{:S(2)}, u32[]{:S(2)}) %all-to-all-start.1) | async-done | bytes 1048608 | tf_op jit(solution)/shard_map/all_to_all | solution.py:38
  181.4 1.2 gather_fusion.1
  182.6 0.9 gather.15
  183.5 0.3 select_bitcast_fusion.1
  183.8 0.2 slice_subtract_fusion.3
  184.0 0.1 copy.19
  184.1 0.2 multiply_add_fusion.2
  184.3 0.1 slice_subtract_fusion.4
  184.4 0.8 fusion.1
  185.2 0.0 all-gather.2.cloned.1.call-update
  185.2 77.6 %all-gather.2.cloned.1.call-done = f32[4,128,4096]{2,0,1:T(4,128)} async-done(((f32[4,4,4096]{2,0,1:T(4,128)}), f32[4,128,4096]{2,0,1:T(4,128)}) %all-gather.2.cloned.1.call-update) | async-done | bytes 8388624 | tf_op jit(solution)/shard_map/all_gather | solution.py:41
  262.8 11.6 %copy.10 = f32[4,128,4096]{2,1,0:T(8,128)} copy(f32[4,128,4096]{2,0,1:T(4,128)} %all-gather.2.cloned.1.call-done) | data formatting | bytes 16777216 | tf_op jit(solution)/shard_map/all_gather | solution.py:41
  (10 shorter events, 0.1 us)
Async XLA Ops:
  14.3 5.3 %copy-start.1 = (s32[32]{0:T(128)S(1)}, s32[32]{0:T(128)}, u32[]{:S(2)}) copy-start(s32[32]{0:T(128)} %param.4) | copy-start | bytes 388
  14.3 5.3 %copy-start.2 = (s32[32]{0:T(128)S(1)}, s32[32]{0:T(128)}, u32[]{:S(2)}) copy-start(s32[32]{0:T(128)} %param.5) | copy-start | bytes 388
  14.3 99.8 %all-to-all-start = ((f32[4,8,16,4096]{3,2,0,1:T(8,128)}), f32[4,8,16,4096]{3,2,0,1:T(8,128)}, u32[]{:S(2)}, u32[]{:S(2)}) async-start(f32[4,8,16,4096]{3,2,0,1:T(8,128)} %copy.8), calls=%async_computation | async-start | bytes 16777216 | tf_op jit(solution)/shard_map/all_to_all | solution.py:34
  141.9 4.7 %copy-start = (f32[8,4,65536]{2,1,0:T(4,128)S(1)}, f32[8,4,65536]{2,1,0:T(4,128)}, u32[]{:S(2)}) copy-start(f32[8,4,65536]{2,1,0:T(4,128)} %select_bitcast_fusion) | copy-start | bytes 25165828
  152.9 28.4 %all-to-all-start.1 = ((f32[4,4,4,4096]{3,2,0,1:T(4,128)}), f32[4,4,4,4096]{3,2,0,1:T(4,128)S(1)}, u32[]{:S(2)}, u32[]{:S(2)}) async-start(f32[4,4,4,4096]{3,2,0,1:T(4,128)} %copy.9), calls=%async_computation.1 | async-start | bytes 2097152 | tf_op jit(solution)/shard_map/all_to_all | solution.py:38
  158.6 104.2 %all-gather.2.cloned.1.call-start = ((), (), s32[]{:S(2)}) async-start(), calls=%async_computation.2 | async-start | bytes 8650752 | tf_op jit(solution)/shard_map/all_gather | solution.py:41
Sparse Core Ops, SparseCore 0:
  185.3 77.3 all-gather.1
where the time goes:
time: 282 us; the launch traced here: 281 us
  waiting for transfers between devices  193 us (68%)
  local copies, waits for them, and re-layouts  46.5 us (16%)
  other arithmetic  17.7 us (6%)
  between operations  13.6 us (5%)
  starting transfers between devices  11 us (4%)
    all_to_all x1, waiting for transfers between devices, local(): lax.all_to_all(bands, 'aa', split_axis=1, concat_axis=1, tiled=True)  93.1 us
    all_gather x1, waiting for transfers between devices, local(): return lax.all_gather(strip, ('aa', 'ba'), axis=1, tiled=True)  77.6 us
    all_to_all x1, waiting for transfers between devices, local(): lax.all_to_all(pieces, 'ba', split_axis=1, concat_axis=1, tiled=True)  21.9 us
    gather x4, local copies, waits for them, and re-layouts, blend_ordered(): ordered = jnp.take(stacked, ordering, axis=1)  20.9 us
    all_gather x1, local copies, waits for them, and re-layouts, local(): return lax.all_gather(strip, ('aa', 'ba'), axis=1, tiled=True)  11.6 us
    transpose x2, other arithmetic, blend_ordered(): jnp.moveaxis(ordered.reshape(channels, count, rows * columns), 1, 0)  9.24 us
    another operation x1, local copies, waits for them, and re-layouts, local(): bands = picture.reshape(4, count_a, rows // count_a, columns)  7.77 us
    all_to_all x1, starting transfers between devices, local(): lax.all_to_all(pieces, 'ba', split_axis=1, concat_axis=1, tiled=True)  5.66 us
  transfers between devices with their start and end apart: 3, of which 3 were waited for; matrix products, arithmetic and copies ran while one was open for 1% of the time, Pallas kernels for 0%

commit v1 on v0

v1 whole, which is shorter than its diff:
```python
import functools

import jax
import jax.numpy as jnp
from jax import lax
from jax.experimental import pallas as pl
from jax.experimental.pallas import tpu as pltpu
from jax.sharding import PartitionSpec as P

MESH = pl.DeviceIdType.MESH
CHUNKS = 8
AHEAD = 2


def kernel(na, nb, nk, depth, brick, img, out, *scratch):
    recv = scratch[:nk]
    zsend = scratch[nk:2 * nk]
    zrecv = scratch[2 * nk:3 * nk]
    (full, order_a, order_b, own_sem, p_send, p_recv, z_send, z_recv,
     x_send, x_recv, g_send, g_recv, d_send, d_recv, out_sem) = scratch[3 * nk:]
    chips = na // 2
    width = recv[0].shape[3]
    wz = width // nb
    a = lax.axis_index("aa")
    b = lax.axis_index("ba")
    chip = a // 2
    core = a % 2
    sibling = chip * 2 + (1 - core)

    barrier = pltpu.get_barrier_semaphore()
    for j in range(1, na):
        pl.semaphore_signal(barrier, inc=1, device_id=(lax.rem(a + j, na), b), device_id_type=MESH)
    for j in range(1, nb):
        pl.semaphore_signal(barrier, inc=1, device_id=(a, lax.rem(b + j, nb)), device_id_type=MESH)
    pl.semaphore_wait(barrier, na + nb - 2)

    def own_copy(k):
        return pltpu.make_async_copy(img.at[:, a, :, pl.ds(k * width, width)], recv[k].at[a], own_sem.at[k])

    def p_copy(k, j, incoming=False):
        other = lax.rem(a + na - j, na) if incoming else lax.rem(a + j, na)
        slot = other if incoming else a
        return pltpu.make_async_remote_copy(
            src_ref=img.at[:, other, :, pl.ds(k * width, width)], dst_ref=recv[k].at[slot],
            send_sem=p_send.at[k, j], recv_sem=p_recv.at[k, j],
            device_id=(other, b), device_id_type=MESH)

    def z_copy(k, j, incoming=False):
        other = lax.rem(b + nb - j, nb) if incoming else lax.rem(b + j, nb)
        slot = other if incoming else b
        return pltpu.make_async_remote_copy(
            src_ref=zsend[k].at[other], dst_ref=zrecv[k].at[slot],
            send_sem=z_send.at[k, j], recv_sem=z_recv.at[k, j],
            device_id=(a, other), device_id_type=MESH)

    def x_copy(k, j, incoming=False):
        other = lax.rem(chip + chips - j, chips) if incoming else lax.rem(chip + j, chips)
        slot = other if incoming else chip
        piece = full.at[k, b, core, :, slot]
        return pltpu.make_async_remote_copy(
            src_ref=piece, dst_ref=piece, send_sem=x_send.at[k, j], recv_sem=x_recv.at[k, j],
            device_id=(other * 2 + core, b), device_id_type=MESH)

    def g_copy(k, j, incoming=False):
        other = lax.rem(b + nb - j, nb) if incoming else lax.rem(b + j, nb)
        slot = other if incoming else b
        piece = full.at[k, slot, core]
        return pltpu.make_async_remote_copy(
            src_ref=piece, dst_ref=piece, send_sem=g_send.at[k, j], recv_sem=g_recv.at[k, j],
            device_id=(a, other), device_id_type=MESH)

    def d_copy(k, j, incoming=False):
        slot = lax.rem(b + nb - j, nb)
        piece = full.at[k, slot, 1 - core if incoming else core]
        return pltpu.make_async_remote_copy(
            src_ref=piece, dst_ref=piece, send_sem=d_send.at[k, j], recv_sem=d_recv.at[k, j],
            device_id=(sibling, b), device_id_type=MESH)

    def out_copy(k, j, c):
        return pltpu.make_async_copy(
            full.at[k, j, c], out.at[:, :, c, :, pl.ds(k * width + j * wz, wz)], out_sem.at[k, j, c])

    def start_first(k):
        for j in range(1, na):
            p_copy(k, j).start()

    def blend(order, count, source, columns):
        total = None
        for position in range(count):
            slot = order[position]
            piece = [source[slot, c, :, columns] for c in range(4)]
            if total is None:
                total = piece
            else:
                left = 1.0 - total[3]
                total = [t + left * p for t, p in zip(total, piece)]
        return total

    for k in range(min(AHEAD, nk)):
        start_first(k)
    for k in range(nk):
        own_copy(k).start()

    ranks = [depth[brick[i * nb + b]] for i in range(na)]
    for position in range(na):
        picked = jnp.int32(0)
        for i in range(1, na):
            picked = jnp.where(lax.rem(ranks[i], na) == position, i, picked)
        order_a[position] = picked
    fronts = [depth[brick[j]] // na for j in range(nb)]
    for position in range(nb):
        picked = jnp.int32(0)
        for j in range(1, nb):
            picked = jnp.where(fronts[j] == position, j, picked)
        order_b[position] = picked

    for step in range(nk + 4):
        k = step
        if 0 <= k < nk:
            own_copy(k).wait()
            for j in range(1, na):
                p_copy(k, j, True).wait_recv()
            for j in range(nb):
                total = blend(order_a, na, recv[k], pl.ds(j * wz, wz))
                for c in range(4):
                    zsend[k][j, c] = total[c]
            for c in range(4):
                zrecv[k][b, c] = zsend[k][b, c]
            for j in range(1, nb):
                z_copy(k, j).start()
        k = step - 1
        if 0 <= k < nk:
            for j in range(1, nb):
                z_copy(k, j, True).wait_recv()
            total = blend(order_b, nb, zrecv[k], pl.ds(0, wz))
            for c in range(4):
                full[k, b, core, c, chip] = total[c]
            for j in range(1, chips):
                x_copy(k, j).start()
        k = step + AHEAD
        if k < nk:
            start_first(k)
        k = step - 2
        if 0 <= k < nk:
            for j in range(1, chips):
                x_copy(k, j, True).wait_recv()
            for j in range(1, nb):
                g_copy(k, j).start()
            d_copy(k, 0).start()
        k = step - 3
        if 0 <= k < nk:
            for j in range(1, nb):
                g_copy(k, j, True).wait_recv()
                d_copy(k, j).start()
        k = step - 4
        if 0 <= k < nk:
            for j in range(nb):
                d_copy(k, j, True).wait_recv()
            for j in range(nb):
                for c in range(2):
                    out_copy(k, j, c).start()
    for k in range(nk):
        for j in range(1, na):
            p_copy(k, j).wait_send()
        for j in range(1, nb):
            z_copy(k, j).wait_send()
            g_copy(k, j).wait_send()
        for j in range(1, chips):
            x_copy(k, j).wait_send()
        for j in range(nb):
            d_copy(k, j).wait_send()
            for c in range(2):
                out_copy(k, j, c).wait()


def local(images, depth, brick_map):
    na = lax.axis_size("aa")
    nb = lax.axis_size("ba")
    rows, columns = images.shape[2], images.shape[3]
    band = rows // na
    nk = min(CHUNKS, columns // (128 * nb))
    width = columns // nk
    wz = width // nb
    chips = na // 2
    dma = pltpu.SemaphoreType.DMA
    f32 = jnp.float32
    scratch = [pltpu.VMEM((na, 4, band, width), f32) for _ in range(nk)]
    scratch += [pltpu.VMEM((nb, 4, band, wz), f32) for _ in range(2 * nk)]
    scratch += [
        pltpu.VMEM((nk, nb, 2, 4, chips, band, wz), f32),
        pltpu.SMEM((na,), jnp.int32), pltpu.SMEM((nb,), jnp.int32),
        dma((nk,)), dma((nk, na)), dma((nk, na)), dma((nk, nb)), dma((nk, nb)),
        dma((nk, chips)), dma((nk, chips)), dma((nk, nb)), dma((nk, nb)),
        dma((nk, nb)), dma((nk, nb)), dma((nk, nb, 2)),
    ]
    smem = pl.BlockSpec(memory_space=pltpu.SMEM)
    hbm = pl.BlockSpec(memory_space=pltpu.MemorySpace.HBM)
    composite = pl.pallas_call(
        functools.partial(kernel, na, nb, nk),
        out_shape=jax.ShapeDtypeStruct((4, chips, 2, band, columns), f32),
        in_specs=[smem, smem, hbm],
        out_specs=hbm,
        scratch_shapes=scratch,
        compiler_params=pltpu.CompilerParams(
            collective_id=0, has_side_effects=True, vmem_limit_bytes=48 * 1024 * 1024),
    )(depth, brick_map, images.reshape(4, na, band, columns))
    return composite.reshape(4, rows, columns)


def solution(mesh):
    placed = (P(("aa", "ba"), None, None, None), P(), P())
    return jax.shard_map(local, mesh=mesh, in_specs=placed, out_specs=P(), check_vma=False)
```

time: 282 us -> 164 us (0.58)
  waiting for transfers between devices: 193 us -> 0 us
  Pallas kernels: 0 us -> 153 us
  local copies, waits for them, and re-layouts: 46.5 us -> 9.08 us
  other arithmetic: 17.7 us -> 0 us
  between operations: 13.6 us -> 0.01 us
  starting transfers between devices: 11 us -> 0 us
    pallas_call x0 -> x1, Pallas kernels: none -> 153 us  [local(): pl.pallas_call(functools.partial(kernel, na, nb, nk), out_shape=jax.Shape...]
    all_to_all x2 -> x0, waiting for transfers between devices: 115 us -> none  [the longest x1 93.1 us: local(): lax.all_to_all(bands, 'aa', split_axis=1, concat_axis=1, tiled=True)]
    all_gather x1 -> x0, waiting for transfers between devices: 77.6 us -> none  [local(): return lax.all_gather(strip, ('aa', 'ba'), axis=1, tiled=True)]
    gather x4 -> x0, local copies, waits for them, and re-layouts: 20.9 us -> none  [blend_ordered(): ordered = jnp.take(stacked, ordering, axis=1)]
    all_gather x1 -> x0, local copies, waits for them, and re-layouts: 11.6 us -> none  [local(): return lax.all_gather(strip, ('aa', 'ba'), axis=1, tiled=True)]
    all_to_all x2 -> x0, starting transfers between devices: 11 us -> none  [the longest x1 5.66 us: local(): lax.all_to_all(pieces, 'ba', split_axis=1, concat_axis=1, tiled=True)]
    another operation x3 -> x0, local copies, waits for them, and re-layouts: 9.7 us -> none  [the longest x1 7.77 us: local(): bands = picture.reshape(4, count_a, rows // count_a, columns)]
    transpose x2 -> x0, other arithmetic: 9.24 us -> none  [blend_ordered(): jnp.moveaxis(ordered.reshape(channels, count, rows * columns), 1, 0)]
  transfers between devices with their start and end apart: 3 -> 0, of which waited for: 3 -> 0; matrix products, arithmetic and copies ran while one was open for 1% -> 0% of each run, Pallas kernels for 0% -> 0%
where the time goes in v1:
time: 164 us; the launch traced here: 162 us
  Pallas kernels  153 us (93%)
  local copies, waits for them, and re-layouts  9.08 us (6%)
    pallas_call x1, Pallas kernels, local(): pl.pallas_call(functools.partial(kernel, na, nb, nk), out_shape=jax.Shape...  153 us
    unnamed x5, local copies, waits for them, and re-layouts  9.08 us

profile of v1, /device:TPU:0, one launch (start us, length us, event | category | flops | bytes accessed | tf_op | source)
XLA Modules:
  0.0 162.1 jit_solution(3056759375627706995)
XLA Ops:
  0.0 0.0 copy-start
  0.0 0.7 copy-done
  0.7 0.0 copy-start.1
  0.7 0.7 copy-done.1
  1.3 153.1 %shard_map.37 = f32[4,4,2,16,4096]{4,3,2,1,0:T(8,128)} custom-call(s32[32]{0:T(128)S(1)} %copy-done, s32[32]{0:T(128)S(1)} %copy-done.1, f32[4,8,16,4096]{3,2,1,0:T(8,128)} %bitcast.3), custom_call_target="tpu_custom_call" | custom-call | tf_op jit(solution)/shard_map/pallas_call | solution.py:198
  154.4 7.8 %copy.5 = f32[4,128,4096]{2,1,0:T(8,128)} copy(f32[4,128,4096]{2,1,0:T(8,128)} %bitcast.2) | data formatting | bytes 16777216
Async XLA Ops:
  0.0 0.7 copy-start
  0.7 0.7 copy-start.1

commit v2 on v1

--- a/solution.py
+++ b/solution.py
@@ -10,6 +10,7 @@
 MESH = pl.DeviceIdType.MESH
 CHUNKS = 8
 AHEAD = 2
+COLUMN_FIRST = 4
 
 
 def kernel(na, nb, nk, depth, brick, img, out, *scratch):
@@ -19,6 +20,9 @@
     (full, order_a, order_b, own_sem, p_send, p_recv, z_send, z_recv,
      x_send, x_recv, g_send, g_recv, d_send, d_recv, out_sem) = scratch[3 * nk:]
     chips = na // 2
+    column_first = range(nk - min(COLUMN_FIRST, nk), nk)
+    strips = [nb if k in column_first else chips for k in range(nk)]
+    blocks = [chips if k in column_first else nb for k in range(nk)]
     width = recv[0].shape[3]
     wz = width // nb
     a = lax.axis_index("aa")
@@ -53,25 +57,43 @@
             send_sem=z_send.at[k, j], recv_sem=z_recv.at[k, j],
             device_id=(a, other), device_id_type=MESH)
 
-    def x_copy(k, j, incoming=False):
-        other = lax.rem(chip + chips - j, chips) if incoming else lax.rem(chip + j, chips)
-        slot = other if incoming else chip
-        piece = full.at[k, b, core, :, slot]
+    def peer_chip(j, incoming):
+        return lax.rem(chip + chips - j, chips) if incoming else lax.rem(chip + j, chips)
+
+    def peer_row(j, incoming):
+        return lax.rem(b + nb - j, nb) if incoming else lax.rem(b + j, nb)
+
+    def strip_copy(k, j, incoming=False):
+        if k in column_first:
+            other = peer_row(j, incoming)
+            piece = full.at[k, other if incoming else b, core, :, chip]
+            target = (a, other)
+        else:
+            other = peer_chip(j, incoming)
+            piece = full.at[k, b, core, :, other if incoming else chip]
+            target = (other * 2 + core, b)
         return pltpu.make_async_remote_copy(
             src_ref=piece, dst_ref=piece, send_sem=x_send.at[k, j], recv_sem=x_recv.at[k, j],
-            device_id=(other * 2 + core, b), device_id_type=MESH)
-
-    def g_copy(k, j, incoming=False):
-        other = lax.rem(b + nb - j, nb) if incoming else lax.rem(b + j, nb)
-        slot = other if incoming else b
-        piece = full.at[k, slot, core]
+            device_id=target, device_id_type=MESH)
+
+    def block(k, slot, side):
+        return full.at[k, :, side, :, slot] if k in column_first else full.at[k, slot, side]
+
+    def block_copy(k, j, incoming=False):
+        if k in column_first:
+            other = peer_chip(j, incoming)
+            target, mine = (other * 2 + core, b), chip
+        else:
+            other = peer_row(j, incoming)
+            target, mine = (a, other), b
+        piece = block(k, other if incoming else mine, core)
         return pltpu.make_async_remote_copy(
             src_ref=piece, dst_ref=piece, send_sem=g_send.at[k, j], recv_sem=g_recv.at[k, j],
-            device_id=(a, other), device_id_type=MESH)
+            device_id=target, device_id_type=MESH)
 
     def d_copy(k, j, incoming=False):
-        slot = lax.rem(b + nb - j, nb)
-        piece = full.at[k, slot, 1 - core if incoming else core]
+        slot = peer_chip(j, True) if k in column_first else peer_row(j, True)
+        piece = block(k, slot, 1 - core if incoming else core)
         return pltpu.make_async_remote_copy(
             src_ref=piece, dst_ref=piece, send_sem=d_send.at[k, j], recv_sem=d_recv.at[k, j],
             device_id=(sibling, b), device_id_type=MESH)
@@ -135,26 +157,26 @@
             total = blend(order_b, nb, zrecv[k], pl.ds(0, wz))
             for c in range(4):
                 full[k, b, core, c, chip] = total[c]
-            for j in range(1, chips):
-                x_copy(k, j).start()
+            for j in range(1, strips[k]):
+                strip_copy(k, j).start()
         k = step + AHEAD
         if k < nk:
             start_first(k)
         k = step - 2
         if 0 <= k < nk:
-            for j in range(1, chips):
-                x_copy(k, j, True).wait_recv()
-            for j in range(1, nb):
-                g_copy(k, j).start()
+            for j in range(1, strips[k]):
+                strip_copy(k, j, True).wait_recv()
+            for j in range(1, blocks[k]):
+                block_copy(k, j).start()
             d_copy(k, 0).start()
         k = step - 3
         if 0 <= k < nk:
-            for j in range(1, nb):
-                g_copy(k, j, True).wait_recv()
+            for j in range(1, blocks[k]):
+                block_copy(k, j, True).wait_recv()
                 d_copy(k, j).start()
         k = step - 4
         if 0 <= k < nk:
-            for j in range(nb):
+            for j in range(blocks[k]):
                 d_copy(k, j, True).wait_recv()
             for j in range(nb):
                 for c in range(2):
@@ -164,11 +186,13 @@
             p_copy(k, j).wait_send()
         for j in range(1, nb):
             z_copy(k, j).wait_send()
-            g_copy(k, j).wait_send()
-        for j in range(1, chips):
-            x_copy(k, j).wait_send()
+        for j in range(1, strips[k]):
+            strip_copy(k, j).wait_send()
+        for j in range(1, blocks[k]):
+            block_copy(k, j).wait_send()
+        for j in range(blocks[k]):
+            d_copy(k, j).wait_send()
         for j in range(nb):
-            d_copy(k, j).wait_send()
             for c in range(2):
                 out_copy(k, j, c).wait()
 
@@ -182,6 +206,7 @@
     width = columns // nk
     wz = width // nb
     chips = na // 2
+    most = max(chips, nb)
     dma = pltpu.SemaphoreType.DMA
     f32 = jnp.float32
     scratch = [pltpu.VMEM((na, 4, band, width), f32) for _ in range(nk)]
@@ -190,8 +215,8 @@
         pltpu.VMEM((nk, nb, 2, 4, chips, band, wz), f32),
         pltpu.SMEM((na,), jnp.int32), pltpu.SMEM((nb,), jnp.int32),
         dma((nk,)), dma((nk, na)), dma((nk, na)), dma((nk, nb)), dma((nk, nb)),
-        dma((nk, chips)), dma((nk, chips)), dma((nk, nb)), dma((nk, nb)),
-        dma((nk, nb)), dma((nk, nb)), dma((nk, nb, 2)),
+        dma((nk, most)), dma((nk, most)), dma((nk, most)), dma((nk, most)),
+        dma((nk, most)), dma((nk, most)), dma((nk, nb, 2)),
     ]
     smem = pl.BlockSpec(memory_space=pltpu.SMEM)
     hbm = pl.BlockSpec(memory_space=pltpu.MemorySpace.HBM)

time: 164 us -> 142 us (0.87)
  Pallas kernels: 153 us -> 132 us
    pallas_call x1, Pallas kernels: 153 us -> 132 us  [local(): pl.pallas_call(functools.partial(kernel, na, nb, nk), out_shape=jax.Shape...]
where the time goes in v2:
time: 142 us; the launch traced here: 141 us
  Pallas kernels  132 us (93%)
  local copies, waits for them, and re-layouts  9.08 us (6%)
    pallas_call x1, Pallas kernels, local(): pl.pallas_call(functools.partial(kernel, na, nb, nk), out_shape=jax.Shape...  132 us
    unnamed x5, local copies, waits for them, and re-layouts  9.08 us

profile of v2, /device:TPU:0, one launch (start us, length us, event | category | flops | bytes accessed | tf_op | source)
XLA Modules:
  0.0 141.3 jit_solution(4546741251716248540)
XLA Ops:
  0.0 0.0 copy-start
  0.0 0.7 copy-done
  0.7 0.0 copy-start.1
  0.7 0.7 copy-done.1
  1.3 132.2 %shard_map.37 = f32[4,4,2,16,4096]{4,3,2,1,0:T(8,128)} custom-call(s32[32]{0:T(128)S(1)} %copy-done, s32[32]{0:T(128)S(1)} %copy-done.1, f32[4,8,16,4096]{3,2,1,0:T(8,128)} %bitcast.3), custom_call_target="tpu_custom_call" | custom-call | tf_op jit(solution)/shard_map/pallas_call | solution.py:223
  133.5 7.8 %copy.5 = f32[4,128,4096]{2,1,0:T(8,128)} copy(f32[4,128,4096]{2,1,0:T(8,128)} %bitcast.2) | data formatting | bytes 16777216
Async XLA Ops:
  0.0 0.7 copy-start
  0.7 0.7 copy-start.1
